TPU v7x, 64 devices: a 2x2x8 block of a 4x4x8 slice. The times are simulated.
64 devices in a mesh: rep: 4 (over x, y), seq: 16 (over z, core).
Axes of the slice: x: 2, y: 2, z: 8, core: 2. Of those that a mesh axis runs over, the one named last changes fastest.
The devices are a block of a 4x4x8 slice.
Arguments:
- hidden: bfloat16 [128, 5120], P('rep'), parts along dimension 0
- w_query: bfloat16 [5120, 4096], replicated
- w_key: bfloat16 [5120, 1024], replicated
- w_value: bfloat16 [5120, 1024], replicated
- w_out: bfloat16 [4096, 5120], P('seq')
- k_cache: bfloat16 [128, 1024, 8, 128], P('rep', 'seq'), parts along dimension 0
- v_cache: bfloat16 [128, 1024, 8, 128], P('rep', 'seq'), parts along dimension 0
- positions: int32 [128], P('rep'), parts along dimension 0
Outputs:
- output 1: bfloat16 [128, 5120], P('rep'), parts along dimension 0
- output 2: bfloat16 [128, 1024, 8, 128], P('rep', 'seq'), parts along dimension 0
- output 3: bfloat16 [128, 1024, 8, 128], P('rep', 'seq'), parts along dimension 0
There are 4 independent parts. A program takes and returns all parts, laid end to end along the dimension named above; an argument that names none is the same for every part.
All inputs are finite; a program needn't handle non-finite values.
Results may differ from a plain program's by a relative error of at most 0.00606072.
Values are sent between devices in bfloat16 or wider.
A program may use at most 768 MiB of HBM per device.

v0:
```python
import jax
import jax.numpy as jnp
from jax import lax
from jax.sharding import PartitionSpec as P


def solution(mesh):
    cache_spec = P('rep', 'seq', None, None)
    in_specs = (P('rep', None), P(), P(), P(), P('seq', None), cache_spec, cache_spec, P('rep'))
    out_specs = (P('rep', None), cache_spec, cache_spec)

    def local_step(hidden, w_query, w_key, w_value, w_out, k_cache, v_cache, positions):
        batch_size, local_len, kv_heads, head_dim = k_cache.shape
        num_heads = w_query.shape[1] // head_dim
        group_size = num_heads // kv_heads
        shard_idx = lax.axis_index('seq')
        q_flat = jnp.dot(hidden, w_query, preferred_element_type=jnp.float32).astype(jnp.bfloat16)
        key_new = jnp.dot(hidden, w_key, preferred_element_type=jnp.float32).astype(jnp.bfloat16).reshape(batch_size, kv_heads, head_dim)
        value_new = jnp.dot(hidden, w_value, preferred_element_type=jnp.float32).astype(jnp.bfloat16).reshape(batch_size, kv_heads, head_dim)
        seq_ids = shard_idx * local_len + jnp.arange(local_len)
        at_pos = (seq_ids[None, :] == positions[:, None])[:, :, None, None]
        k_updated = jnp.where(at_pos, key_new[:, None], k_cache)
        v_updated = jnp.where(at_pos, value_new[:, None], v_cache)
        is_valid = (seq_ids[None, :] <= positions[:, None])[:, None, None, :]
        q_heads = q_flat.reshape(batch_size, kv_heads, group_size, head_dim)
        scores = jnp.einsum('bkgd,bskd->bkgs', q_heads, k_updated, preferred_element_type=jnp.float32) * head_dim ** -0.5
        scores = jnp.where(is_valid, scores, -jnp.inf)
        local_max = jnp.max(scores, axis=-1)
        safe_max = jnp.where(jnp.isfinite(local_max), local_max, 0.0)
        weights = jnp.exp(scores - safe_max[..., None])
        local_sum = jnp.sum(weights, axis=-1)
        local_out = jnp.einsum('bkgs,bskd->bkgd', weights.astype(jnp.bfloat16), v_updated, preferred_element_type=jnp.float32)
        global_max = lax.pmax(local_max, 'seq')
        rescale = jnp.exp(local_max - global_max)
        total_sum, total_out = lax.psum((local_sum * rescale, local_out * rescale[..., None]), 'seq')
        combined = (total_out / total_sum[..., None]).astype(jnp.bfloat16).reshape(batch_size, num_heads * head_dim)
        row_count = w_out.shape[0]
        combined_rows = lax.dynamic_slice_in_dim(combined, shard_idx * row_count, row_count, axis=1)
        part_out = jnp.dot(combined_rows, w_out, preferred_element_type=jnp.float32)
        result = lax.psum(part_out, 'seq').astype(jnp.bfloat16)
        return result, k_updated, v_updated

    return jax.shard_map(local_step, mesh=mesh, in_specs=in_specs, out_specs=out_specs, check_vma=False)
```

profile of v0, /device:TPU:21, one launch (start us, length us, event | category | flops | bytes accessed | tf_op | source)
XLA Modules:
  0.0 269.4 jit_solution(9658526429834809410)
XLA Ops:
  7.2 0.0 copy-start
  7.2 0.1 all-reduce.3.cloned.1.call-start
  7.3 0.0 copy-start.1
  7.3 0.0 copy-start.2
  7.3 6.1 %fusion.13 = bf16[4,8,8,128]{3,1,2,0:T(8,128)(2,1)S(1)} fusion(bf16[32,5120]{1,0:T(8,128)(2,1)} %param.8, bf16[5120,1024]{1,0:T(8,128)(2,1)} %param.10), kind=kOutput, calls=%fused_computation.12 | convolution fusion | flops 335577088 | bytes 10878976 | tf_op jit(solution)/shard_map/dot_general | solution.py:18
  13.5 1.0 copy-done.1
  14.5 1.9 fusion.14
  16.4 16.7 %convolution_convert_fusion = bf16[32,4096]{1,0:T(8,128)(2,1)S(1)} fusion(bf16[32,5120]{1,0:T(8,128)(2,1)S(1)} %copy-done.2, bf16[5120,4096]{1,0:T(8,128)(2,1)} %param.9), kind=kOutput, calls=%fused_computation | convolution fusion | flops 1342308352 | bytes 42532864 | tf_op jit(solution)/shard_map/dot_general | solution.py:17
  33.1 0.9 reshape.73
  34.0 0.1 broadcast_compare_fusion.1
  34.1 8.5 %broadcast_select_fusion.1 = (bf16[32,64,8,128]{3,2,1,0:T(8,128)(2,1)S(1)}, bf16[32,64,8,128]{3,2,1,0:T(8,128)(2,1)}) fusion(bf16[32,64,8,128]{3,2,1,0:T(8,128)(2,1)} %param.13, pred[32,64]{1,0:T(8,128)(4,1)S(1)} %get-tuple-element.8, bf16[32,8,128]{2,1,0:T(8,128)(2,1)S(1)} %bitcast.14, bf16[32,64,8,128]{3,2,1,0:T(8,128)(2,1)} %param.14, ...), kind=kLoop, calls=%fused_computation.6 | loop fusion | flops 4194304 | bytes 16910336 | tf_op jit(solution)/shard_map/jit(_where)/select_n | solution.py:22
  42.6 2.0 copy-done.3
  44.6 2.3 fusion.23
  47.0 0.0 copy-start.4
  47.0 51.1 %pmax.7 = f32[32,8,4]{2,1,0:T(8,128)S(1)} all-reduce(f32[32,8,4]{2,1,0:T(8,128)S(1)} %get-tuple-element.9), channel_id=1, replica_groups=mesh['rep'=4,'seq'=16] {'seq'}, use_global_device_ids=true, to_apply=%region_1.2 | all-reduce | flops 1024 | bytes 8192 | tf_op jit(solution)/shard_map/pmax | solution.py:33
  98.2 0.7 fusion.15
  98.9 4.4 %fusion.7 = f32[32,8,4,128]{3,2,1,0:T(4,128)} fusion(bf16[32,64,8,128]{3,2,1,0:T(8,128)(2,1)} %get-tuple-element.6, f32[32,8,4,64]{3,2,1,0:T(4,128)S(1)} %get-tuple-element.10, f32[32,8,4]{2,1,0:T(8,128)S(1)} %get-tuple-element.4, f32[32,8,4]{2,1,0:T(8,128)} %copy-done.4), kind=kOutput, calls=%fused_computation.8 | convolution fusion | flops 17039360 | bytes 4988928 | tf_op jit(solution)/shard_map/bkgs,bskd->bkgd/dot_general | solution.py:32
  103.3 0.1 all-reduce.3.cloned.1.call-update
  103.3 46.5 %psum.22 = f32[32,8,4]{2,1,0:T(8,128)S(1)} all-reduce(f32[32,8,4]{2,1,0:T(8,128)S(1)} %get-tuple-element.3), channel_id=1, replica_groups=mesh['rep'=4,'seq'=16] {'seq'}, use_global_device_ids=true, to_apply=%region_4.5 | all-reduce | flops 1024 | bytes 8192 | tf_op jit(solution)/shard_map/psum | solution.py:35
  149.8 57.8 %all-reduce.3.cloned.1.call-done = f32[32,8,4,128]{3,2,1,0:T(4,128)} async-done(((f32[32,8,4,128]{3,2,1,0:T(4,128)}), f32[32,8,4,128]{3,2,1,0:T(4,128)}) %all-reduce.3.cloned.1.call-update) | async-done | bytes 524304 | tf_op jit(solution)/shard_map/psum | solution.py:35
  207.7 1.4 divide_convert_fusion
  209.1 0.2 reshape.74
  209.3 0.6 fusion.19
  209.8 52.8 %all-reduce.4 = bf16[32,5120]{1,0:T(8,128)(2,1)} all-reduce(f32[32,5120]{1,0:T(8,128)S(1)} %fusion.19), channel_id=1, replica_groups=mesh['rep'=4,'seq'=16] {'seq'}, use_global_device_ids=true, to_apply=%region_5.6 | all-reduce | flops 163840 | bytes 983040 | tf_op jit(solution)/shard_map/psum | solution.py:40
  (13 shorter events, 0.1 us)
Async XLA Ops:
  7.2 202.1 %copy-start = (bf16[256,5120]{1,0:T(8,128)(2,1)S(1)}, bf16[256,5120]{1,0:T(8,128)(2,1)}, u32[]{:S(2)}) copy-start(bf16[256,5120]{1,0:T(8,128)(2,1)} %param.12) | copy-start | bytes 7864324
  7.2 200.5 %all-reduce.3.cloned.1.call-start = ((), (), s32[]{:S(2)}) async-start(), calls=%async_computation | async-start | bytes 1048576 | tf_op jit(solution)/shard_map/psum | solution.py:35
  7.3 7.2 %copy-start.1 = (bf16[5120,1024]{1,0:T(8,128)(2,1)S(1)}, bf16[5120,1024]{1,0:T(8,128)(2,1)}, u32[]{:S(2)}) copy-start(bf16[5120,1024]{1,0:T(8,128)(2,1)} %param.11) | copy-start | bytes 31457284
  7.3 7.2 %copy-start.2 = (bf16[32,5120]{1,0:T(8,128)(2,1)S(1)}, bf16[32,5120]{1,0:T(8,128)(2,1)}, u32[]{:S(2)}) copy-start(bf16[32,5120]{1,0:T(8,128)(2,1)} %param.8) | copy-start | bytes 983044
  16.4 17.6 %copy-start.6 = (s32[32]{0:T(128)S(1)}, s32[32]{0:T(128)}, u32[]{:S(2)}) copy-start(s32[32]{0:T(128)} %param.15) | copy-start | bytes 388
  34.1 10.6 %copy-start.5 = (bf16[32,8,4,128]{3,2,1,0:T(4,128)(2,1)S(1)}, bf16[32,8,4,128]{3,2,1,0:T(4,128)(2,1)}, u32[]{:S(2)}) copy-start(bf16[32,8,4,128]{3,2,1,0:T(4,128)(2,1)} %reshape.73) | copy-start | bytes 786436
  42.6 2.0 copy-start.3
  47.0 51.2 %copy-start.4 = (f32[32,8,4]{2,1,0:T(8,128)}, f32[32,8,4]{2,1,0:T(8,128)S(1)}, u32[]{:S(2)}) copy-start(f32[32,8,4]{2,1,0:T(8,128)S(1)} %is-finite_select_fusion) | copy-start | bytes 12292
Sparse Core Ops, SparseCore 0:
  103.4 104.1 all-reduce.2
where the time goes:
time: 272 us; the launch traced here: 269 us
  blocking collectives  150 us (55%)
  waiting for transfers between devices  57.9 us (21%)
  matrix products  32 us (12%)
  between operations  14.2 us (5%)
  other arithmetic  10.7 us (4%)
  local copies, waits for them, and re-layouts  4.17 us (2%)
    psum x1, waiting for transfers between devices, local_step(): lax.psum((local_sum * rescale, local_out * rescale[..., None]), 'seq')  57.8 us
    psum x1, blocking collectives, local_step(): result = lax.psum(part_out, 'seq').astype(jnp.bfloat16)  52.8 us
    pmax x1, blocking collectives, local_step(): global_max = lax.pmax(local_max, 'seq')  51.1 us
    psum x1, blocking collectives, local_step(): lax.psum((local_sum * rescale, local_out * rescale[..., None]), 'seq')  46.5 us
    dot_general x1, matrix products, local_step(): jnp.dot(hidden, w_query, preferred_element_type=jnp.float32)  16.7 us
    select_n x1, other arithmetic, local_step(): k_updated = jnp.where(at_pos, key_new[:, None], k_cache)  8.54 us
    dot_general x1, matrix products, local_step(): jnp.dot(hidden, w_key, preferred_element_type=jnp.float32)  6.13 us
  transfers between devices with their start and end apart: 1, of which 1 were waited for; matrix products, arithmetic and copies ran while one was open for 0% of the time, Pallas kernels for 0%

commit v1 on v0

v1 whole, which is shorter than its diff:
```python
import functools

import jax
import jax.numpy as jnp
from jax import lax
from jax.experimental import pallas as pl
from jax.experimental.pallas import tpu as pltpu
from jax.sharding import PartitionSpec as P

MESH = pl.DeviceIdType.MESH
BF16 = jnp.bfloat16
F32 = jnp.float32
NEG = float('-inf')
DMA = pltpu.SemaphoreType.DMA
NT = (((1,), (1,)), ((), ()))


def place(n_chips):
    me = lax.axis_index('seq')
    chip = lax.div(me, 2)
    core = lax.rem(me, 2)
    return chip, core, me + 1 - 2 * core


def remote(src, dst, send, recv, dev):
    return pltpu.make_async_remote_copy(src_ref=src, dst_ref=dst, send_sem=send, recv_sem=recv,
                                        device_id={'seq': dev}, device_id_type=MESH)


def greet(peers):
    barrier = pltpu.get_barrier_semaphore()
    for p in peers:
        pl.semaphore_signal(barrier, inc=1, device_id={'seq': p}, device_id_type=MESH)
    return lambda: pl.semaphore_wait(barrier, len(peers))


def project_kernel(n_chips, pieces, width, x_hbm, wq, wk, wv, k_hbm, v_hbm, g_ref, k_out, v_out,
                   x_ref, wbuf, xsem, wsem, csem, send_sem, recv_sem):
    chip, core, sibling = place(n_chips)
    parity = lax.rem(chip, 2)
    shard = 2 * parity + core
    right = lax.rem(chip + 1, n_chips)
    left = lax.rem(chip + n_chips - 1, n_chips)
    arrived = greet([sibling, 2 * right, 2 * right + 1, 2 * left, 2 * left + 1])
    nq = pieces - 2

    def load(p):
        src, col = (wq, (shard * nq + p) * width) if p < nq else ((wk, wv)[p - nq], shard * width)
        return pltpu.make_async_copy(src.at[:, pl.ds(pl.multiple_of(col, 128), width)], wbuf.at[p], wsem.at[p])

    load_x = pltpu.make_async_copy(x_hbm, x_ref, xsem)
    load_x.start()
    ahead = 3
    for p in range(ahead):
        load(p).start()
    caches = [pltpu.make_async_copy(k_hbm, k_out, csem.at[0]), pltpu.make_async_copy(v_hbm, v_out, csem.at[1])]
    load_x.wait()
    x = x_ref[...]
    sends = []
    for p in range(pieces):
        load(p).wait()
        if p + ahead < pieces:
            load(p + ahead).start()
        elif p + ahead - pieces < 2:
            caches[p + ahead - pieces].start()
        acc = jnp.dot(x, wbuf[p], preferred_element_type=F32)
        g_ref[shard, p] = acc.astype(BF16)
        if p == 0:
            arrived()
        block = g_ref.at[shard, p]
        near = right if p % 2 == 0 else left
        for s, (dev, slot) in enumerate([(sibling, 0), (2 * near, 1 + core), (2 * near + 1, 1 + core)]):
            copy = remote(block, block, send_sem.at[p, s], recv_sem.at[p, slot], dev)
            copy.start()
            sends.append(copy)
    for p in range(pieces):
        for s in range(3):
            owner = 2 * parity + 1 - core if s == 0 else 2 * (1 - parity) + s - 1
            block = g_ref.at[owner, p]
            remote(block, block, send_sem.at[p, s], recv_sem.at[p, s], sibling).wait_recv()
    for copy in sends:
        copy.wait_send()
    for copy in caches:
        copy.wait()


def patch_kernel(length, kv_heads, pos_ref, g_ref, k_in, v_in, k_ref, v_ref, rows):
    batch = k_ref.shape[0]
    dim = k_ref.shape[-1]
    shards, pieces = g_ref.shape[:2]
    per = kv_heads // shards
    base = lax.axis_index('seq') * length
    for kind in range(2):
        for h in range(kv_heads):
            part = g_ref[h // per, pieces - 2 + kind]
            lo = (h % per) * dim
            rows[kind, pl.ds(h, batch, stride=kv_heads), :] = part[:, lo:lo + dim].astype(F32)
    for b in range(batch):
        p = pos_ref[b] - base

        @pl.when((p >= 0) & (p < length))
        def _():
            for kind, ref in ((0, k_ref), (1, v_ref)):
                ref[b, p] = rows[kind, kv_heads * b:kv_heads * (b + 1), :].astype(BF16)


MSG = 72


def attend_kernel(n_chips, kv_heads, scale, length, pos_ref, g_ref, k_ref, v_ref, wo_hbm, y_ref,
                  qs, tmat, obuf, sbuf, mbuf, rbuf, wo, ybuf, ysib, yc, yr, yg, wsem,
                  sa_s, sa_r, sb_s, sb_r, ya_s, ya_r, yb_s, yb_r, ag_s, ag_r, fw_s, fw_r):
    chip, core, sibling = place(n_chips)
    batch, span, dim = k_ref.shape
    heads = 4 * n_chips
    order = sorted(range(1, n_chips), key=lambda d: -min(d, n_chips - d))
    peer = {d: lax.rem(chip + d, n_chips) for d in range(1, n_chips)}
    source = {d: lax.rem(chip + n_chips - d, n_chips) for d in range(1, n_chips)}
    arrived = greet([sibling] + [2 * peer[d] + core for d in order])
    load_wo = pltpu.make_async_copy(wo_hbm, wo, wsem)
    load_wo.start()
    base = lax.axis_index('seq') * length

    half = heads // 2
    per = heads // g_ref.shape[0]
    wide = g_ref.shape[-1]
    for h in range(heads):
        col = (h % per) * dim
        part = g_ref[h // per, col // wide]
        r = (h % 2) * half + h // 2
        qs[pl.ds(r, batch, stride=heads), :] = part[:, col % wide:col % wide + dim].astype(F32)
    row = lax.broadcasted_iota(jnp.int32, (heads, span), 0)
    col = lax.broadcasted_iota(jnp.int32, (heads, span), 1)
    same = lax.div(lax.rem(row, half), heads // kv_heads // 2) == lax.rem(col, kv_heads)
    tmat[...] = jnp.where(same, lax.div(col, kv_heads), 1 << 20)
    lane = lax.broadcasted_iota(jnp.int32, (heads, dim), 1)

    unroll = 4

    def group(i, carry):
        mst, lst = carry
        for u in range(unroll):
            b = i * unroll + u
            q = qs[pl.ds(pl.multiple_of(b * heads, 8), heads), :].astype(BF16)
            s = lax.dot_general(q, k_ref[b], NT, preferred_element_type=F32) * scale
            s = jnp.where(tmat[...] <= pos_ref[b] - base, s, NEG)
            m = jnp.max(s, axis=1, keepdims=True)
            p = jnp.exp(s - jnp.where(m == NEG, 0.0, m))
            l = jnp.sum(p, axis=1, keepdims=True)
            o = jnp.dot(p.astype(BF16), v_ref[b], preferred_element_type=F32)
            mst = jnp.where(lane == b, m, mst)
            lst = jnp.where(lane == b, l, lst)
            obuf[pl.ds(b, half, stride=MSG), :] = o[:half]
            obuf[pl.ds(b + batch, half, stride=MSG), :] = o[half:]
        return mst, lst

    zero = jnp.zeros((heads, dim), F32)
    mst, lst = lax.fori_loop(0, batch // unroll, group, (zero, zero))
    stat = 2 * batch
    for r, v in enumerate((mst[:half], mst[half:], lst[:half], lst[half:])):
        obuf[pl.ds(stat + r, half, stride=MSG), :] = v
    for r in range(4, 8):
        obuf[pl.ds(stat + r, half, stride=MSG), :] = jnp.zeros((half, dim), F32)
    arrived()

    def message(j):
        return obuf.at[pl.ds(pl.multiple_of(j * MSG, 8), MSG)]

    pair = []
    for t in range(n_chips):
        copy = remote(message(2 * t + 1 - core), sbuf.at[t], sa_s.at[t], sa_r.at[t], sibling)
        copy.start()
        pair.append(copy)
    sub = lax.broadcasted_iota(jnp.int32, (8, dim), 0)
    scales = []
    for t in range(n_chips):
        pair[t].wait_recv()
        mine = obuf[pl.ds(pl.multiple_of((2 * t + core) * MSG + stat, 8), 8), :]
        theirs = sbuf[t, stat:, :]
        top = jnp.maximum(mine, theirs)
        safe = jnp.where(top == NEG, 0.0, top)
        a0, a1 = jnp.exp(mine - safe), jnp.exp(theirs - safe)
        total = pltpu.roll(a0, 2, 0) * mine + pltpu.roll(a1, 2, 0) * theirs
        mbuf[t, stat:, :] = jnp.where(sub < 2, top, jnp.where(sub < 4, total, 0.0))
        scales += [a0, a1]
    cols = jnp.concatenate(scales, axis=0).T
    for t in range(n_chips):
        for hh in range(2):
            lo = hh * batch
            own = obuf[pl.ds(pl.multiple_of((2 * t + core) * MSG + lo, 8), batch), :]
            c = 16 * t + hh
            mbuf[t, lo:lo + batch, :] = (own * cols[:batch, c:c + 1]
                                         + sbuf[t, lo:lo + batch, :] * cols[:batch, c + 8:c + 9])

    sends = []
    for d in order:
        copy = remote(mbuf.at[peer[d]], rbuf.at[chip], sb_s.at[d], sb_r.at[d], 2 * peer[d] + core)
        copy.start()
        sends.append(copy)
    rbuf[chip] = mbuf[chip]
    for d in order:
        remote(mbuf.at[source[d]], rbuf.at[source[d]], sb_s.at[d], sb_r.at[d], 2 * source[d] + core).wait_recv()
    stats = [rbuf[t, stat:, :] for t in range(n_chips)]
    top = functools.reduce(jnp.maximum, stats)
    fac = [jnp.exp(v - top) for v in stats]
    total = functools.reduce(jnp.add, [a * pltpu.roll(v, 6, 0) for a, v in zip(fac, stats)])
    cols = jnp.concatenate([a / total for a in fac] + [jnp.zeros((128 - 8 * n_chips, dim), F32)], axis=0).T
    outs = []
    for hh in range(2):
        lo = hh * batch
        outs.append(functools.reduce(jnp.add, [
            rbuf[t, lo:lo + batch, :] * cols[:batch, 8 * t + hh:8 * t + hh + 1] for t in range(n_chips)]))
    combined = jnp.concatenate(outs, axis=1).astype(BF16)
    for copy in pair + sends:
        copy.wait_send()

    load_wo.wait()
    quarter = ybuf.shape[-1]
    rows = ybuf.shape[2]

    def product(q):
        cut = wo[:, pl.ds(pl.multiple_of(q * quarter, 128), quarter)]
        out = jnp.dot(combined, cut, preferred_element_type=F32)
        return out.reshape(batch // rows, rows, quarter)

    pair = []
    for e in range(2):
        q = 2 * (1 - core) + e
        ybuf[q] = product(q)
        copy = remote(ybuf.at[q], ysib.at[e], ya_s.at[e], ya_r.at[e], sibling)
        copy.start()
        pair.append(copy)
    groups = batch // rows
    for e in range(2):
        q = 2 * core + e
        ybuf[q] = product(q)
    for e in range(2):
        pair[e].wait_recv()
        yc[groups * e:groups * (e + 1)] = ybuf[2 * core + e] + ysib[e]
    sends = []
    for d in order:
        copy = remote(yc.at[peer[d]], yr.at[chip], yb_s.at[d], yb_r.at[d], 2 * peer[d] + core)
        copy.start()
        sends.append(copy)
    acc = yc[chip]
    for d in order:
        remote(yc.at[source[d]], yr.at[source[d]], yb_s.at[d], yb_r.at[d], 2 * source[d] + core).wait_recv()
        acc = acc + yr[source[d]]
    yg[core, chip] = acc.astype(BF16)
    for copy in pair + sends:
        copy.wait_send()

    sends = []
    piece = yg.at[core, chip]
    for d in order:
        copy = remote(piece, piece, ag_s.at[d], ag_r.at[d], 2 * peer[d] + core)
        copy.start()
        sends.append(copy)
    copy = remote(piece, piece, fw_s.at[0], fw_r.at[0], sibling)
    copy.start()
    sends.append(copy)
    for d in order:
        got = yg.at[core, source[d]]
        remote(got, got, ag_s.at[d], ag_r.at[d], 2 * source[d] + core).wait_recv()
        copy = remote(got, got, fw_s.at[d], fw_r.at[d], sibling)
        copy.start()
        sends.append(copy)
    for d in [0] + order:
        got = yg.at[1 - core, chip if d == 0 else source[d]]
        remote(got, got, fw_s.at[d], fw_r.at[d], sibling).wait_recv()
    for k in range(2):
        for t in range(n_chips):
            q = 2 * k + t // groups
            lo = rows * (t % groups)
            y_ref[lo:lo + rows, q * quarter:(q + 1) * quarter] = yg[k, t]
    for copy in sends:
        copy.wait_send()


def solution(mesh):
    cache_spec = P('rep', 'seq', None, None)
    in_specs = (P('rep', None), P(), P(), P(), P('seq', None), cache_spec, cache_spec, P('rep'))
    out_specs = (P('rep', None), cache_spec, cache_spec)
    n_seq = mesh.shape['seq']
    n_chips = n_seq // 2

    def local_step(hidden, w_query, w_key, w_value, w_out, k_cache, v_cache, positions):
        batch, length, kv_heads, dim = k_cache.shape
        model, q_width = w_query.shape
        heads = q_width // dim
        width = kv_heads * dim // 4
        nq = q_width // 4 // width
        pieces = nq + 2
        vm = pl.BlockSpec(memory_space=pltpu.VMEM)
        hbm = pl.BlockSpec(memory_space=pltpu.HBM)
        smem = pl.BlockSpec(memory_space=pltpu.SMEM)
        stay = lambda a: pltpu.with_memory_space_constraint(a, pltpu.HBM)
        gathered, k_held, v_held = pl.pallas_call(
            functools.partial(project_kernel, n_chips, pieces, width),
            out_shape=(pltpu.VMEM((4, pieces, batch, width), BF16),
                       pltpu.VMEM(k_cache.shape, BF16), pltpu.VMEM(v_cache.shape, BF16)),
            in_specs=[hbm] * 6,
            out_specs=(vm, vm, vm),
            scratch_shapes=[pltpu.VMEM(hidden.shape, BF16), pltpu.VMEM((pieces, model, width), BF16),
                            DMA, DMA((pieces,)), DMA((2,)),
                            DMA((pieces, 3)), DMA((pieces, 3))],
            compiler_params=pltpu.CompilerParams(collective_id=0, has_side_effects=True, vmem_limit_bytes=40 << 20),
            name='project',
        )(*map(stay, (hidden, w_query, w_key, w_value, k_cache, v_cache)))

        k_new, v_new = pl.pallas_call(
            functools.partial(patch_kernel, length, kv_heads),
            out_shape=(pltpu.VMEM(k_cache.shape, BF16), pltpu.VMEM(v_cache.shape, BF16)),
            in_specs=[smem, vm, vm, vm],
            out_specs=(vm, vm),
            scratch_shapes=[pltpu.VMEM((2, batch * kv_heads, dim), F32)],
            input_output_aliases={2: 0, 3: 1},
            compiler_params=pltpu.CompilerParams(vmem_limit_bytes=32 << 20),
            name='patch',
        )(positions, gathered, k_held, v_held)

        rows = batch * 4 // n_chips // 2
        quarter = model // 4
        span = length * kv_heads
        f = lambda *shape: pltpu.VMEM(shape, F32)
        result = pl.pallas_call(
            functools.partial(attend_kernel, n_chips, kv_heads, dim ** -0.5, length),
            out_shape=jax.ShapeDtypeStruct((batch, model), BF16),
            in_specs=[smem, vm, vm, vm, hbm],
            out_specs=vm,
            scratch_shapes=[
                f(heads * batch, dim), pltpu.VMEM((heads, span), jnp.int32),
                f(n_seq * MSG, dim), f(n_chips, MSG, dim), f(n_chips, MSG, dim), f(n_chips, MSG, dim),
                pltpu.VMEM(w_out.shape, BF16),
                f(4, batch // rows, rows, quarter), f(2, batch // rows, rows, quarter),
                f(n_chips, rows, quarter), f(n_chips, rows, quarter),
                pltpu.VMEM((2, n_chips, rows, quarter), BF16), DMA,
            ] + [DMA((n_chips,))] * 4 + [DMA((2,))] * 2 + [DMA((n_chips,))] * 6,
            compiler_params=pltpu.CompilerParams(collective_id=1, has_side_effects=True, vmem_limit_bytes=40 << 20),
            name='attend',
        )(positions, gathered, k_new.reshape(batch, span, dim), v_new.reshape(batch, span, dim), stay(w_out))
        return result, k_new, v_new

    return jax.shard_map(local_step, mesh=mesh, in_specs=in_specs, out_specs=out_specs, check_vma=False)
```

time: 272 us -> 63.5 us (0.23)
  blocking collectives: 150 us -> 0 us
  Pallas kernels: 0 us -> 57.9 us
  waiting for transfers between devices: 57.9 us -> 0 us
  matrix products: 32 us -> 0 us
  between operations: 14.2 us -> 0.67 us
  other arithmetic: 10.7 us -> 0 us
    psum x2 -> x0, blocking collectives: 99.3 us -> none  [the longest x1 52.8 us: local_step(): result = lax.psum(part_out, 'seq').astype(jnp.bfloat16)]
    pallas_call x0 -> x3, Pallas kernels: none -> 57.9 us  [the longest x1 39.8 us: local_step(): pl.pallas_call(functools.partial(attend_kernel, n_chips, kv_heads, dim **...]
    psum x1 -> x0, waiting for transfers between devices: 57.8 us -> none  [local_step(): lax.psum((local_sum * rescale, local_out * rescale[..., None]), 'seq')]
    pmax x1 -> x0, blocking collectives: 51.1 us -> none  [local_step(): global_max = lax.pmax(local_max, 'seq')]
    dot_general x6 -> x0, matrix products: 32 us -> none  [the longest x1 16.7 us: local_step(): jnp.dot(hidden, w_query, preferred_element_type=jnp.float32)]
    select_n x2 -> x0, other arithmetic: 8.55 us -> none  [the longest x1 8.54 us: local_step(): k_updated = jnp.where(at_pos, key_new[:, None], k_cache)]
  transfers between devices with their start and end apart: 1 -> 0, of which waited for: 1 -> 0; matrix products, arithmetic and copies ran while one was open for 0% -> 0% of each run, Pallas kernels for 0% -> 0%
where the time goes in v1:
time: 63.5 us; the launch traced here: 63.3 us
  Pallas kernels  57.9 us (91%)
  local copies, waits for them, and re-layouts  4.76 us (7%)
  between operations  0.67 us (1%)
    pallas_call x1, Pallas kernels, local_step(): pl.pallas_call(functools.partial(attend_kernel, n_chips, kv_heads, dim **...  39.8 us
    pallas_call x1, Pallas kernels, local_step(): pl.pallas_call(functools.partial(project_kernel, n_chips, pieces, width),...  17.2 us
    unnamed x5, local copies, waits for them, and re-layouts  4.76 us

profile of v1, /device:TPU:21, one launch (start us, length us, event | category | flops | bytes accessed | tf_op | source)
XLA Modules:
  0.0 63.3 jit_solution(16278166061203895086)
XLA Ops:
  0.6 0.0 copy-start
  0.6 17.2 %project.1 = (bf16[4,6,32,256]{3,2,1,0:T(8,128)(2,1)S(1)}, bf16[32,64,8,128]{3,2,1,0:T(8,128)(2,1)S(1)}, bf16[32,64,8,128]{3,2,1,0:T(8,128)(2,1)S(1)}) custom-call(bf16[32,5120]{1,0:T(8,128)(2,1)} %x_hbm.1, bf16[5120,4096]{1,0:T(8,128)(2,1)} %wq.1, bf16[5120,1024]{1,0:T(8,128)(2,1)} %wk.1, bf16[5120,1024]{1,0:T(8,128)(2,1)} %wv.1, ...), custom_call_target="tpu_custom_call" | custom-call | tf_op jit(solution)/shard_map/project/pallas_call | solution.py:298
  17.8 0.0 copy-done
  17.9 0.9 %patch.1 = (bf16[32,64,8,128]{3,2,1,0:T(8,128)(2,1)S(1)}, bf16[32,64,8,128]{3,2,1,0:T(8,128)(2,1)S(1)}) custom-call(s32[32]{0:T(128)S(1)} %copy-done, bf16[4,6,32,256]{3,2,1,0:T(8,128)(2,1)S(1)} %get-tuple-element.8.g_ref, bf16[32,64,8,128]{3,2,1,0:T(8,128)(2,1)S(1)} %get-tuple-element.9.k_in, ...), custom_call_target="tpu_custom_call", output_to_operand_aliasing={{0}: (2, {}), {1}: (3, {})} | custom-call | tf_op jit(solution)/shard_map/patch/pallas_call | solution.py:311
  18.7 39.8 %attend.1 = bf16[32,5120]{1,0:T(8,128)(2,1)S(1)} custom-call(s32[32]{0:T(128)S(1)} %copy-done, bf16[4,6,32,256]{3,2,1,0:T(8,128)(2,1)S(1)} %get-tuple-element.8.g_ref, bf16[32,512,128]{2,1,0:T(8,128)(2,1)S(1)} %bitcast.2, bf16[32,512,128]{2,1,0:T(8,128)(2,1)S(1)} %bitcast.3, bf16[256,5120]{1,0:T(8,128)(2,1)} %wo_hbm.1), custom_call_target="tpu_custom_call" | custom-call | tf_op jit(solution)/shard_map/attend/pallas_call | solution.py:326
  58.6 2.0 %copy.18 = bf16[32,64,8,128]{3,2,1,0:T(8,128)(2,1)} copy(bf16[32,64,8,128]{3,2,1,0:T(8,128)(2,1)S(1)} %get-tuple-element.14) | data formatting | bytes 8388608
  60.6 2.0 %copy.19 = bf16[32,64,8,128]{3,2,1,0:T(8,128)(2,1)} copy(bf16[32,64,8,128]{3,2,1,0:T(8,128)(2,1)S(1)} %get-tuple-element.15) | data formatting | bytes 8388608
  62.6 0.7 %copy.20 = bf16[32,5120]{1,0:T(8,128)(2,1)} copy(bf16[32,5120]{1,0:T(8,128)(2,1)S(1)} %attend.1) | data formatting | bytes 655360
Async XLA Ops:
  0.6 17.2 %copy-start = (s32[32]{0:T(128)S(1)}, s32[32]{0:T(128)}, u32[]{:S(2)}) copy-start(s32[32]{0:T(128)} %pos_ref.3) | copy-start | bytes 388
